TPU v7x, 256 devices: a 2x2x32 block of a 4x8x32 slice. The times are simulated.
256 devices in a mesh: member: 4 (over y, x), wave: 64 (over z, core).
Axes of the slice: x: 2, y: 2, z: 32, core: 2. Of those that a mesh axis runs over, the one named last changes fastest.
The devices are a block of a 4x8x32 slice.
Arguments:
- vorticity: bfloat16 [5120, 32, 1280], P(('member', 'wave')), parts along dimension 0, may hold values from -6 to 6
- divergence: bfloat16 [5120, 32, 1280], P(('member', 'wave')), parts along dimension 0, may hold values from -6 to 6
- legendre: bfloat16 [1280, 64, 1280], P('wave'), may hold values from -0.0068359375 to 0.0068359375
- wave_of_slot: int32 [1280], replicated, may hold values from 0 to 1279, as said below
- cycle_points: int32 [64], P('wave'), may hold values from 20 to 5136, as said below
- cos_squared: float32 [64], P('wave'), may hold values from 0.25 to 1
Outputs:
- grid: bfloat16 [256, 96, 5136], P(('member', 'wave')), parts along dimension 0
There are 4 independent parts, one for each index of `member`. A program takes and returns all parts, laid end to end along the dimension named above; an argument that names none is the same for every part. Nothing has to cross between parts.
Inputs may be any that keep to these rules, and one draw needn't show every extreme that they name: `wave_of_slot`: each wavenumber appears in exactly one slot. `cycle_points`: every count is a multiple of 4; some cycle has 5136 points.
All inputs are finite; a program needn't handle non-finite values.
Results may differ from a plain program's by a relative error of at most 0.0063.
Values may be sent and summed in bfloat16 or wider, within the bound.
A program may use at most 128 MiB of HBM per device.

v0:
```python
import jax
import jax.numpy as jnp
from jax import lax
from jax.sharding import Mesh
from jax.sharding import PartitionSpec as P

NWAVE = 1280
NLON = 5136
WAVE = ("wave_0", "wave_1")
MEMBER_WAVE = ("member", "wave_0", "wave_1")


def split_up(array, dim, size):
    lengths = array.shape
    pieces = array.reshape(*lengths[:dim], size, lengths[dim] // size, *lengths[dim + 1 :])
    return jnp.moveaxis(pieces, dim, 0)


def laid_out(pieces, dim):
    lengths = list(pieces.shape[1:])
    lengths[dim] *= pieces.shape[0]
    return jnp.moveaxis(pieces, 0, dim).reshape(lengths)


def moved_by_axis(pieces, axes, sequence):
    inside = pieces.shape[1:]
    filled = pieces.reshape(*(lax.axis_size(a) for a in axes), *inside)
    for k in sequence:
        filled = lax.all_to_all(filled, axes[k], k, k, tiled=True)
    return filled.reshape(-1, *inside)


def two_step_exchange(array, groups, sequence, split_dim, concat_dim):
    size = lax.axis_size(groups[0]) * lax.axis_size(groups[1])
    pieces = split_up(array, split_dim, size)
    return laid_out(moved_by_axis(pieces, groups, sequence), concat_dim)


def spectral_fields(zeta_in, delta_in, waves):
    columns = zeta_in.shape[-1]
    levels = zeta_in.shape[1] // 2
    degree = waves[:, None] + jnp.arange(columns, dtype=jnp.int32)[None, :]
    living = degree < NWAVE
    positive = living & (degree > 0)
    wave_f = waves.astype(jnp.float32)[:, None]
    degree_f = degree.astype(jnp.float32)
    radius = NWAVE / 4.0
    inverse = jnp.where(positive, -radius / jnp.maximum(degree_f * (degree_f + 1.0), 1.0), 0.0)
    quotient = jnp.maximum(degree_f * degree_f - wave_f * wave_f, 0.0) / jnp.maximum(
        4.0 * degree_f * degree_f - 1.0, 1.0
    )
    coupling = jnp.where(positive, jnp.sqrt(quotient), 0.0)
    coupling_next = jnp.concatenate([coupling[:, 1:], jnp.zeros_like(coupling[:, :1])], axis=1)
    upper_coef = ((degree_f + 2.0) * coupling_next)[:, None, :]
    lower_coef = ((degree_f - 1.0) * coupling)[:, None, :]
    live_mask = living.astype(jnp.float32)[:, None, :]
    zeta = zeta_in.astype(jnp.float32) * live_mask
    delta = delta_in.astype(jnp.float32) * live_mask
    stream = zeta * inverse[:, None, :]
    potential = delta * inverse[:, None, :]

    def meridional(values):
        shifted_up = jnp.concatenate([values[..., 1:], jnp.zeros_like(values[..., :1])], axis=-1)
        shifted_down = jnp.concatenate([jnp.zeros_like(values[..., :1]), values[..., :-1]], axis=-1)
        return (upper_coef * shifted_up - lower_coef * shifted_down) * live_mask

    stream_h = meridional(stream)
    potential_h = meridional(potential)
    wave_three = waves.astype(jnp.float32)[:, None, None]
    u_real = -wave_three * potential[:, levels:] - stream_h[:, :levels]
    u_imag = wave_three * potential[:, :levels] - stream_h[:, levels:]
    v_real = -wave_three * stream[:, levels:] + potential_h[:, :levels]
    v_imag = wave_three * stream[:, :levels] + potential_h[:, levels:]
    return jnp.concatenate([u_real, u_imag, v_real, v_imag, zeta, delta], axis=1).astype(
        jnp.bfloat16
    )


def derive(fourier, waves, cosine_sq):
    cycles, slots, columns = fourier.shape
    levels = columns // 8
    groups = fourier.reshape(cycles, slots, 4, 2, levels)
    wind_u = groups[:, :, 0]
    wind_v = groups[:, :, 1]
    zeta_f = groups[:, :, 2]
    delta_f = groups[:, :, 3]
    scale = (waves.astype(jnp.float32) / (NWAVE / 4.0))[None, :, None]
    u_lon = jnp.stack([-scale * wind_u[:, :, 1], scale * wind_u[:, :, 0]], axis=2)
    v_lon = jnp.stack([-scale * wind_v[:, :, 1], scale * wind_v[:, :, 0]], axis=2)
    factor = cosine_sq[:, None, None, None]
    u_lat = v_lon / factor - zeta_f
    v_lat = delta_f - u_lon / factor
    stacked = jnp.stack([wind_u, wind_v, u_lon, v_lon, u_lat, v_lat], axis=2)
    return stacked.reshape(cycles, slots, 12 * levels)


def cycle_basis(waves, points):
    positions = jnp.arange(NLON, dtype=jnp.int32)
    phase = waves[:, None] * positions[None, :] % points
    theta = 2.0 * jnp.pi / points.astype(jnp.float32) * phase.astype(jnp.float32)
    keeping = (2 * waves[:, None] < points) & (positions[None, :] < points)
    weight = jnp.where(waves == 0, 1.0, 2.0)[:, None]
    cosine = jnp.where(keeping, weight * jnp.cos(theta), 0.0)
    sine = jnp.where(keeping, -weight * jnp.sin(theta), 0.0)
    return jnp.stack([cosine, sine]).astype(jnp.bfloat16)


def synthesize(fields, waves, points, pieces):
    slot_count = fields.shape[1]
    levels = fields.shape[2] // 12
    span = slot_count // pieces

    def one_cycle(item):
        cycle_fields, count = item
        packed = cycle_fields.astype(jnp.bfloat16).reshape(slot_count, 6, 2, levels)

        def add_segment(index, summed):
            start = index * span
            segment = lax.dynamic_slice_in_dim(packed, start, span, 0)
            segment_waves = lax.dynamic_slice_in_dim(waves, start, span, 0)
            basis = cycle_basis(segment_waves, count)
            return summed + jnp.einsum(
                "sfrl,rsp->flp", segment, basis, preferred_element_type=jnp.float32
            )

        summed = lax.fori_loop(0, pieces, add_segment, jnp.zeros((6, levels, NLON), jnp.float32))
        return summed.reshape(6 * levels, NLON)

    return lax.map(one_cycle, (fields, points))


def body(vorticity, divergence, legendre, wave_of_slot, cycle_points, cos_squared):
    slot_count = vorticity.shape[0]
    offset = lax.axis_index(WAVE) * slot_count
    own_waves = lax.dynamic_slice_in_dim(wave_of_slot, offset, slot_count, 0)
    spec = spectral_fields(vorticity, divergence, own_waves)
    fourier = jnp.einsum("sck,slk->lsc", spec, legendre, preferred_element_type=jnp.float32)
    arrived = two_step_exchange(fourier, ("wave_0", "wave_1"), (1, 0), 0, 1)
    fields = derive(arrived, wave_of_slot, cos_squared)
    summed = synthesize(fields, wave_of_slot, cycle_points, 4)
    return summed.astype(jnp.bfloat16)


def solution(mesh):
    finer = Mesh(mesh.devices.reshape(mesh.shape["member"], 32, 2), ("member", "wave_0", "wave_1"))
    in_specs = (
        P(MEMBER_WAVE, None, None),
        P(MEMBER_WAVE, None, None),
        P(WAVE, None, None),
        P(),
        P(WAVE),
        P(WAVE),
    )
    out_specs = P(MEMBER_WAVE, None, None)
    return jax.shard_map(body, mesh=finer, in_specs=in_specs, out_specs=out_specs, check_vma=False)
```

profile of v0, /device:TPU:37, one launch (start us, length us, event | category | flops | bytes accessed | tf_op | source)
XLA Modules:
  0.0 566.9 jit_solution(12358632999225854633)
XLA Ops:
  2.1 5.6 fusion.18
  7.6 11.4 %fusion.58 = (f32[20,32,1279]{2,1,0:T(8,128)}, f32[20,32,1279]{2,1,0:T(8,128)}, f32[20,32,1279]{2,1,0:T(8,128)}, f32[20,32,1279]{2,1,0:T(8,128)}) fusion(f32[20,32,1280]{2,1,0:T(8,128)} %get-tuple-element.229, f32[20,32,1280]{2,1,0:T(8,128)} %get-tuple-element.230), kind=kLoop, calls=%fused_computation.100 | loop fusion | bytes 26193920 | tf_op jit(solution)/shard_map/slice | solution.py:63
  19.1 6.0 %subtract_multiply_fusion = (f32[20,32,1280]{2,1,0:T(8,128)S(1)}, f32[20,32,1280]{2,1,0:T(8,128)S(1)}) fusion(f32[20,32,1279]{2,1,0:T(8,128)} %get-tuple-element.222, f32[20,32,1279]{2,1,0:T(8,128)} %get-tuple-element.221, f32[20,1280]{1,0:T(8,128)S(1)} %get-tuple-element.250, f32[20,1280]{1,0:T(8,128)} %get-tuple-element.253, f32[20,1280]{1,0:T(8,128)S(1)} %fusion.43, ...), kind=kLoop, calls=%fused_computation.24 | loop fusion | flops 6553600 | bytes 19957760 | tf_op jit(solution)/shard_map/mul | solution.py:65
  25.5 1.5 copy-done.1
  27.5 1.0 copy-done.3
  29.4 2.3 fusion.60
  31.8 24.3 %all_to_all.10 = f32[32,2,1,20,128]{4,0,3,2,1:T(8,128)S(1)} all-to-all(f32[32,2,1,20,128]{4,0,3,2,1:T(8,128)S(1)} %copy.9), channel_id=1, replica_groups=mesh['member'=4,'wave_0'=32,'wave_1'=2] {'wave_1'}, dimensions={1} | all-to-all | bytes 1310720 | tf_op jit(solution)/shard_map/all_to_all | solution.py:29
  56.1 1.3 copy.10
  57.5 13.4 %all-to-all-start.1 = ((f32[32,2,1,20,128]{4,1,3,2,0:T(2,128)}), f32[32,2,1,20,128]{4,1,3,2,0:T(2,128)}, u32[]{:S(2)}, u32[]{:S(2)}) async-start(f32[32,2,1,20,128]{4,1,3,2,0:T(2,128)} %copy.10), calls=%async_computation.1 | async-start | bytes 1310720 | tf_op jit(solution)/shard_map/all_to_all | solution.py:29
  72.3 73.6 %all-to-all-done.1 = f32[32,2,1,20,128]{4,1,3,2,0:T(2,128)} async-done(((f32[32,2,1,20,128]{4,1,3,2,0:T(2,128)}), f32[32,2,1,20,128]{4,1,3,2,0:T(2,128)}, u32[]{:S(2)}, u32[]{:S(2)}) %all-to-all-start.1) | async-done | bytes 655392 | tf_op jit(solution)/shard_map/all_to_all | solution.py:29
  145.8 5.9 %copy.11 = f32[32,2,1,20,128]{3,1,0,4,2:T(2,128)} copy(f32[32,2,1,20,128]{4,1,3,2,0:T(2,128)} %all-to-all-done.1) | data formatting | bytes 1310720 | tf_op jit(solution)/shard_map/all_to_all | solution.py:29
  151.7 6.6 %reshape_reshape_transpose_reshape.3 = f32[1,1280,4,2,16]{1,4,3,2,0:T(8,128)} reshape(f32[32,2,1,20,128]{3,1,0,4,2:T(2,128)} %copy.11) | data formatting | bytes 1310720 | tf_op jit(solution)/shard_map/reshape;reshape;transpose;reshape | solution.py:82
  158.3 1.0 slice_bitcast_fusion
  159.3 1.0 fusion.29
  163.1 401.2 %while.23 = (s32[]{:T(128)}, f32[6,16,5136]{2,1,0:T(8,128)}, bf16[1280,6,2,16]{0,3,2,1:T(8,128)(2,1)}, s32[1280]{0:T(1024)S(1)}, s32[]{:T(128)}, /*index=5*/f32[...) while((s32[]{:T(128)}, f32[6,16,5136]{2,1,0:T(8,128)}, ...), condition=%wide.region_1.2_spmd.clone, body=%wide.region_0.1_spmd.clone.sunk | while | flops 663332032 | bytes 17449060 | solution.py:126
  164.5 92.5 %fusion.69 = (bf16[1,320,5136]{2,1,0:T(8,128)(2,1)}, bf16[1,320,5136]{2,1,0:T(8,128)(2,1)}) fusion(s32[]{:T(128)} %get-tuple-element.344, s32[320]{0:T(512)S(1)} %get-tuple-element.310, f32[]{:T(128)} %get-tuple-element.343, f32[320]{0:T(512)S(1)} %get-tuple-element.311, pred[]{:T(512)} %get-tuple-element.345, ...), kind=kLoop, calls=%fused_computation.5.clone.1 | loop fusion | flops 27939840 | bytes 6583385 | tf_op jit(solution)/shard_map/convert
  257.0 6.0 %fusion.70 = f32[6,16,5136]{2,1,0:T(8,128)} fusion(bf16[1,320,5136]{2,1,0:T(8,128)(2,1)} %get-tuple-element.312, bf16[1,320,5136]{2,1,0:T(8,128)(2,1)} %get-tuple-element.313, f32[6,16,5136]{2,1,0:T(8,128)} %get-tuple-element.327, pred[]{:T(512)S(6)} %compare.8, bf16[1280,6,2,16]{0,3,2,1:T(8,128)(2,1)} %get-tuple-element.340, s32[]{:T(128)S(6)} %select_n.147), kind=kOutput, calls=%fused_computation.4.clone.1 | convolution fusion | flops 635384832 | bytes 10852357 | tf_op jit(solution)/shard_map/while/body/eval_jaxpr/while/body/eval_jaxpr/sfrl,rsp->flp/dot_general | solution.py:122
  264.4 92.5 %fusion.69 = (bf16[1,320,5136]{2,1,0:T(8,128)(2,1)}, bf16[1,320,5136]{2,1,0:T(8,128)(2,1)}) fusion(s32[]{:T(128)} %get-tuple-element.344, s32[320]{0:T(512)S(1)} %get-tuple-element.310, f32[]{:T(128)} %get-tuple-element.343, f32[320]{0:T(512)S(1)} %get-tuple-element.311, pred[]{:T(512)} %get-tuple-element.345, ...), kind=kLoop, calls=%fused_computation.5.clone.1 | loop fusion | flops 27939840 | bytes 6583385 | tf_op jit(solution)/shard_map/convert
  356.9 6.6 %fusion.70 = f32[6,16,5136]{2,1,0:T(8,128)} fusion(bf16[1,320,5136]{2,1,0:T(8,128)(2,1)} %get-tuple-element.312, bf16[1,320,5136]{2,1,0:T(8,128)(2,1)} %get-tuple-element.313, f32[6,16,5136]{2,1,0:T(8,128)} %get-tuple-element.327, pred[]{:T(512)S(6)} %compare.8, bf16[1280,6,2,16]{0,3,2,1:T(8,128)(2,1)} %get-tuple-element.340, s32[]{:T(128)S(6)} %select_n.147), kind=kOutput, calls=%fused_computation.4.clone.1 | convolution fusion | flops 635384832 | bytes 10852357 | tf_op jit(solution)/shard_map/while/body/eval_jaxpr/while/body/eval_jaxpr/sfrl,rsp->flp/dot_general | solution.py:122
  364.8 92.5 %fusion.69 = (bf16[1,320,5136]{2,1,0:T(8,128)(2,1)}, bf16[1,320,5136]{2,1,0:T(8,128)(2,1)}) fusion(s32[]{:T(128)} %get-tuple-element.344, s32[320]{0:T(512)S(1)} %get-tuple-element.310, f32[]{:T(128)} %get-tuple-element.343, f32[320]{0:T(512)S(1)} %get-tuple-element.311, pred[]{:T(512)} %get-tuple-element.345, ...), kind=kLoop, calls=%fused_computation.5.clone.1 | loop fusion | flops 27939840 | bytes 6583385 | tf_op jit(solution)/shard_map/convert
  457.3 6.6 %fusion.70 = f32[6,16,5136]{2,1,0:T(8,128)} fusion(bf16[1,320,5136]{2,1,0:T(8,128)(2,1)} %get-tuple-element.312, bf16[1,320,5136]{2,1,0:T(8,128)(2,1)} %get-tuple-element.313, f32[6,16,5136]{2,1,0:T(8,128)} %get-tuple-element.327, pred[]{:T(512)S(6)} %compare.8, bf16[1280,6,2,16]{0,3,2,1:T(8,128)(2,1)} %get-tuple-element.340, s32[]{:T(128)S(6)} %select_n.147), kind=kOutput, calls=%fused_computation.4.clone.1 | convolution fusion | flops 635384832 | bytes 10852357 | tf_op jit(solution)/shard_map/while/body/eval_jaxpr/while/body/eval_jaxpr/sfrl,rsp->flp/dot_general | solution.py:122
  465.3 92.5 %fusion.69 = (bf16[1,320,5136]{2,1,0:T(8,128)(2,1)}, bf16[1,320,5136]{2,1,0:T(8,128)(2,1)}) fusion(s32[]{:T(128)} %get-tuple-element.344, s32[320]{0:T(512)S(1)} %get-tuple-element.310, f32[]{:T(128)} %get-tuple-element.343, f32[320]{0:T(512)S(1)} %get-tuple-element.311, pred[]{:T(512)} %get-tuple-element.345, ...), kind=kLoop, calls=%fused_computation.5.clone.1 | loop fusion | flops 27939840 | bytes 6583385 | tf_op jit(solution)/shard_map/convert
  557.8 6.6 %fusion.70 = f32[6,16,5136]{2,1,0:T(8,128)} fusion(bf16[1,320,5136]{2,1,0:T(8,128)(2,1)} %get-tuple-element.312, bf16[1,320,5136]{2,1,0:T(8,128)(2,1)} %get-tuple-element.313, f32[6,16,5136]{2,1,0:T(8,128)} %get-tuple-element.327, pred[]{:T(512)S(6)} %compare.8, bf16[1280,6,2,16]{0,3,2,1:T(8,128)(2,1)} %get-tuple-element.340, s32[]{:T(128)S(6)} %select_n.147), kind=kOutput, calls=%fused_computation.4.clone.1 | convolution fusion | flops 635384832 | bytes 10852357 | tf_op jit(solution)/shard_map/while/body/eval_jaxpr/while/body/eval_jaxpr/sfrl,rsp->flp/dot_general | solution.py:122
  564.3 2.6 convert_element_type.99
  (48 shorter events, 12.1 us)
Async XLA Ops:
  0.0 29.4 %copy-start = (bf16[20,64,1280]{2,1,0:T(8,128)(2,1)S(1)}, bf16[20,64,1280]{2,1,0:T(8,128)(2,1)}, u32[]{:S(2)}) copy-start(bf16[20,64,1280]{2,1,0:T(8,128)(2,1)} %param.10) | copy-start | bytes 9830404
  19.1 6.0 %copy-start.2 = (f32[20,32,1280]{2,1,0:T(8,128)S(1)}, f32[20,32,1280]{2,1,0:T(8,128)}, u32[]{:S(2)}) copy-start(f32[20,32,1280]{2,1,0:T(8,128)} %get-tuple-element.229) | copy-start | bytes 9830404
  25.1 1.9 copy-start.1
  27.0 1.4 copy-start.3
  27.2 1.8 copy-start.4
  31.7 40.5 %copy-start.6 = (s32[1280]{0:T(1024)S(1)}, s32[1280]{0:T(1024)}, u32[]{:S(2)}) copy-start(s32[1280]{0:T(1024)} %param.11) | copy-start | bytes 15364
  57.5 88.4 %all-to-all-start.1 = ((f32[32,2,1,20,128]{4,1,3,2,0:T(2,128)}), f32[32,2,1,20,128]{4,1,3,2,0:T(2,128)}, u32[]{:S(2)}, u32[]{:S(2)}) async-start(f32[32,2,1,20,128]{4,1,3,2,0:T(2,128)} %copy.10), calls=%async_computation.1 | async-start | bytes 1310720 | tf_op jit(solution)/shard_map/all_to_all | solution.py:29
  162.3 0.8 copy-start.5
where the time goes:
time: 568 us; the launch traced here: 567 us
  other arithmetic  395 us (70%)
  waiting for transfers between devices  73.6 us (13%)
  local copies, waits for them, and re-layouts  30.9 us (5%)
  matrix products  28 us (5%)
  blocking collectives  24.3 us (4%)
  starting transfers between devices  13.4 us (2%)
    another operation x4, other arithmetic  370 us
    all_to_all x1, waiting for transfers between devices, moved_by_axis(): filled = lax.all_to_all(filled, axes[k], k, k, tiled=True)  73.6 us
    dot_general x4, matrix products, add_segment(): jnp.einsum('sfrl,rsp->flp', segment, basis, preferred_element_type=jnp.fl...  25.7 us
    all_to_all x1, blocking collectives, moved_by_axis(): filled = lax.all_to_all(filled, axes[k], k, k, tiled=True)  24.3 us
    all_to_all x1, starting transfers between devices, moved_by_axis(): filled = lax.all_to_all(filled, axes[k], k, k, tiled=True)  13.4 us
    slice x1, local copies, waits for them, and re-layouts, meridional(): values[..., 1:]  11.4 us
  transfers between devices with their start and end apart: 1, of which 1 were waited for; matrix products, arithmetic and copies ran while one was open for 0% of the time, Pallas kernels for 0%

commit v1 on v0

v1 whole, which is shorter than its diff:
```python
import functools

import jax
import jax.numpy as jnp
from jax import lax
from jax.experimental import pallas as pl
from jax.experimental.pallas import tpu as pltpu
from jax.sharding import PartitionSpec as P

NLON = 5136
MESH = pl.DeviceIdType.MESH
F32 = jnp.float32
BF16 = jnp.bfloat16
LANES = 128
NBLOCK = 768
NPAD = -(-NLON // NBLOCK) * NBLOCK
HEAD = 16
GROUP = 16
NT = (((1,), (1,)), ((), ()))


def partner(r, z, c, chips, sign):
    q = r // 2
    x = r % 2
    d = jnp.where(q % 2 == 1, (q + 1) // 2, chips - q // 2)
    chip = (z + 2 * chips + sign * d) % chips
    return chip * 2 + (c + x) % 2


def kernel(
    vort, div, leg, wave, points, cosq, out,
    spec, legv, mown, coef_a, coef_b, coef_c, res,
    send_a, send_b, recv_a, recv_b, mb, basis, fields, acc,
    in_sem, ssem, rsem_a, rsem_b,
    *, n, nwave,
):
    w = lax.axis_index("wave")
    z = w // 2
    c = w % 2
    chips = n // 2
    slots = vort.shape[0]
    rows = vort.shape[1]
    half = rows // 2
    tail = slots - HEAD
    radius = nwave / 4.0
    steps = in_sem.shape[0]
    per = slots // steps
    groups = n // GROUP
    ka = GROUP * HEAD

    def loads(g):
        at = pl.ds(g * per, per)
        return (
            pltpu.make_async_copy(vort.at[at], spec.at[at, pl.ds(2 * rows, rows)], in_sem.at[g, 0]),
            pltpu.make_async_copy(div.at[at], spec.at[at, pl.ds(3 * rows, rows)], in_sem.at[g, 1]),
            pltpu.make_async_copy(leg.at[at], legv.at[at], in_sem.at[g, 2]),
        )

    for g in range(steps):
        for copy in loads(g):
            copy.start()

    barrier = pltpu.get_barrier_semaphore()

    def greet(r, carry):
        pl.semaphore_signal(
            barrier, inc=1, device_id={"wave": partner(r, z, c, chips, -1)}, device_id_type=MESH
        )
        return carry

    lax.fori_loop(1, n, greet, 0)

    mown[...] = jnp.zeros_like(mown)
    for s in range(slots):
        mown[s : s + 1, :] = jnp.full((1, LANES), wave[w * slots + s].astype(F32), F32)
    m_own = mown[...]
    lane = lax.broadcasted_iota(jnp.int32, m_own.shape, 1).astype(F32)

    def coupled(deg):
        quotient = jnp.maximum(deg * deg - m_own * m_own, 0.0) / (4.0 * deg * deg - 1.0)
        return -radius * jnp.sqrt(quotient) / deg

    for j in range(nwave // LANES):
        cols = slice(j * LANES, (j + 1) * LANES)
        deg = m_own + (lane + float(j * LANES))
        safe = jnp.maximum(deg, 1.0)
        live = deg < float(nwave)
        coef_a[:, cols] = jnp.where(live & (deg >= 1.0), -radius * m_own / (safe * (safe + 1.0)), 0.0)
        coef_b[:, cols] = jnp.where(deg + 1.0 < float(nwave), coupled(deg + 1.0), 0.0)
        coef_c[:, cols] = jnp.where(live & (deg >= 2.0), coupled(safe), 0.0)

    lane16 = lax.broadcasted_iota(jnp.int32, (16, nwave), 1)

    def one_slot(s, carry):
        m = wave[w * slots + s]
        a = coef_a[pl.ds(s, 1), :]
        b = coef_b[pl.ds(s, 1), :]
        cc = coef_c[pl.ds(s, 1), :]
        parts = []
        for i in range(4):
            x = spec[s, pl.ds(2 * rows + half * i, half), :].astype(F32)
            up = pltpu.roll(x, nwave - 1, 1)
            down = pltpu.roll(x, 1, 1)
            parts.append((x * a, up * b - down * cc))
        (zr, hzr), (zi, hzi), (dr, hdr), (di, hdi) = parts
        spec[s, pl.ds(0, half), :] = (-di - hzr).astype(BF16)
        spec[s, pl.ds(half, half), :] = (dr - hzi).astype(BF16)
        spec[s, pl.ds(2 * half, half), :] = (-zi + hdr).astype(BF16)
        spec[s, pl.ds(3 * half, half), :] = (zr + hdi).astype(BF16)
        mask = jnp.where(lane16 < nwave - m, 1.0, 0.0).astype(BF16)
        values = legv[s]
        masked = jnp.concatenate([values[16 * i : 16 * i + 16] * mask for i in range(n // 16)], axis=0)
        res[pl.ds(pl.multiple_of(s * n, n), n), :] = lax.dot_general(
            masked, spec[s], NT, preferred_element_type=F32
        )
        return carry

    for g in range(steps):
        for copy in loads(g):
            copy.wait()
        lax.fori_loop(g * per, (g + 1) * per, one_slot, 0)

    def pack(r, carry):
        dst = partner(r, z, c, chips, -1)
        send_a[r] = res[pl.ds(dst, HEAD, stride=n), :].astype(BF16)
        send_b[r] = res[pl.ds(HEAD * n + dst, tail, stride=n), :].astype(BF16)
        return carry

    lax.fori_loop(0, n, pack, 0)
    recv_a[0] = send_a[0]
    recv_b[0] = send_b[0]

    pl.semaphore_wait(barrier, n - 1)

    def post_b(j, carry):
        r = n - 1 - j
        pltpu.make_async_remote_copy(
            src_ref=send_b.at[r], dst_ref=recv_b.at[r], send_sem=ssem.at[1], recv_sem=rsem_b,
            device_id={"wave": partner(r, z, c, chips, -1)}, device_id_type=MESH,
        ).start()
        return carry

    def post_a(j, carry):
        r = n - 1 - j
        pltpu.make_async_remote_copy(
            src_ref=send_a.at[r], dst_ref=recv_a.at[r], send_sem=ssem.at[0], recv_sem=rsem_a.at[r // GROUP],
            device_id={"wave": partner(r, z, c, chips, -1)}, device_id_type=MESH,
        ).start()
        return carry

    lax.fori_loop(0, n - 1, post_b, 0)
    lax.fori_loop(0, n - 1, post_a, 0)

    def place(r, carry):
        base = partner(r, z, c, chips, 1) * slots
        for s in range(HEAD):
            mb[pl.ds(r * HEAD + s, 1), :] = jnp.full((1, LANES), wave[base + s].astype(F32), F32)
        for s in range(tail):
            mb[pl.ds(n * HEAD + r * tail + s, 1), :] = jnp.full(
                (1, LANES), wave[base + HEAD + s].astype(F32), F32
            )
        return carry

    lax.fori_loop(0, n, place, 0)

    count = points[0].astype(F32)
    pv = jnp.full((1, LANES), count, F32)
    ip = 1.0 / pv

    def turn(x):
        t = (x - jnp.floor(x * ip + 0.5) * pv) * ip
        u = t * 3.14159265358979
        v = u * u
        sn = u * (1.0 + v * (-1.0 / 6 + v * (1.0 / 120 + v * (-1.0 / 5040 + v * (1.0 / 362880 - v / 39916800)))))
        cs = 1.0 + v * (
            -0.5 + v * (1.0 / 24 + v * (-1.0 / 720 + v * (1.0 / 40320 + v * (-1.0 / 3628800 + v / 479001600))))
        )
        return 1.0 - 2.0 * sn * sn, 2.0 * sn * cs

    span = 32

    def make_basis(i, carry):
        m = mb[pl.ds(pl.multiple_of(i * span, span), span), :]
        pos = lax.broadcasted_iota(jnp.int32, m.shape, 1).astype(F32)
        c0, s0 = turn(m * pos)
        cr, sr = turn(m * float(LANES))
        weight = jnp.where(m == 0.0, 1.0, 2.0)
        weight = jnp.where(2.0 * m < pv, weight, 0.0)
        cv = weight * c0
        sv = -weight * s0
        g = i // (ka // span)
        at = pl.multiple_of((i % (ka // span)) * span, span)
        for j in range(NPAD // LANES):
            cols = slice(j * LANES, (j + 1) * LANES)
            basis[g, pl.ds(at, span), cols] = cv.astype(BF16)
            basis[g, pl.ds(at + ka, span), cols] = sv.astype(BF16)
            cv, sv = cv * cr + sv * sr, sv * cr - cv * sr
        return carry

    lax.fori_loop(0, mb.shape[0] // span, make_basis, 0)

    eye = (
        lax.broadcasted_iota(jnp.int32, (LANES, LANES), 0) == lax.broadcasted_iota(jnp.int32, (LANES, LANES), 1)
    ).astype(F32).astype(BF16)
    first = (lax.broadcasted_iota(jnp.int32, (8, LANES), 1) == 0).astype(F32)
    inv_c = 1.0 / jnp.full((1, ka), cosq[0], F32)

    def derive(g, arrived):
        mrow = lax.dot_general(
            first, mb[pl.ds(g * ka, ka), :], NT, precision=lax.Precision.HIGHEST, preferred_element_type=F32
        )
        q = mrow[0:1] / radius
        x = lax.dot_general(eye, arrived, NT, preferred_element_type=F32)
        ur, ui, vr, vi, zr, zi, dr, di = (x[half * i : half * (i + 1)] for i in range(8))
        for side, (u, v, ul, vl, zt, dl) in enumerate(
            ((ur, vr, -q * ui, -q * vi, zr, dr), (ui, vi, q * ur, q * vr, zi, di))
        ):
            parts = (u, v, ul, vl, vl * inv_c - zt, dl - ul * inv_c)
            for f, part in enumerate(parts):
                fields[half * f : half * (f + 1), ka * side : ka * (side + 1)] = part.astype(BF16)

    def accumulate(g, opening):
        def column(j, carry):
            at = pl.ds(pl.multiple_of(j * NBLOCK, NBLOCK), NBLOCK)
            new = jnp.dot(fields[...], basis[g, :, at], preferred_element_type=F32)
            acc[:, at] = new if opening else acc[:, at] + new
            return carry

        lax.fori_loop(0, NPAD // NBLOCK, column, 0)

    pltpu.make_async_copy(recv_b.at[pl.ds(1, n - 1)], recv_b.at[pl.ds(1, n - 1)], rsem_b).wait()
    derive(groups, recv_b[...].reshape(n * tail, LANES))
    accumulate(groups, True)
    for g in range(groups - 1, -1, -1):
        at = pl.ds(1, GROUP - 1) if g == 0 else pl.ds(g * GROUP, GROUP)
        pltpu.make_async_copy(recv_a.at[at], recv_a.at[at], rsem_a.at[g]).wait()
        derive(g, recv_a[pl.ds(g * GROUP, GROUP)].reshape(ka, LANES))
        if g > 0:
            accumulate(g, False)

    for j in range(NPAD // NBLOCK):
        lo = j * NBLOCK
        hi = min(lo + NBLOCK, NLON)
        new = jnp.dot(fields[...], basis[0, :, lo : lo + NBLOCK], preferred_element_type=F32)
        total = acc[:, lo : lo + NBLOCK] + new
        pos = lax.broadcasted_iota(jnp.int32, total.shape, 1) + lo
        out[0, :, lo:hi] = jnp.where(pos < points[0], total, 0.0).astype(BF16)[:, : hi - lo]

    pltpu.make_async_copy(send_a.at[pl.ds(1, n - 1)], send_a.at[pl.ds(1, n - 1)], ssem.at[0]).wait()
    pltpu.make_async_copy(send_b.at[pl.ds(1, n - 1)], send_b.at[pl.ds(1, n - 1)], ssem.at[1]).wait()


def solution(mesh):
    n = mesh.shape["wave"]

    def body(vort, div, leg, wave, points, cosq):
        slots, rows, nwave = vort.shape
        tail = slots - HEAD
        fields = 12 * rows // 4
        hbm = pl.BlockSpec(memory_space=pl.ANY)
        smem = pl.BlockSpec(memory_space=pltpu.SMEM)
        groups = n // GROUP
        own = -(-slots // 8) * 8
        return pl.pallas_call(
            functools.partial(kernel, n=n, nwave=nwave),
            out_shape=jax.ShapeDtypeStruct((1, fields, NLON), BF16),
            in_specs=[hbm, hbm, hbm, smem, smem, smem],
            out_specs=pl.BlockSpec(memory_space=pltpu.VMEM),
            scratch_shapes=[
                pltpu.VMEM((slots, 4 * rows, nwave), BF16),
                pltpu.VMEM((slots, n, nwave), BF16),
                pltpu.VMEM((own, LANES), F32),
                pltpu.VMEM((own, nwave), F32),
                pltpu.VMEM((own, nwave), F32),
                pltpu.VMEM((own, nwave), F32),
                pltpu.VMEM((slots * n, LANES), F32),
                pltpu.VMEM((n, HEAD, LANES), BF16),
                pltpu.VMEM((n, tail, LANES), BF16),
                pltpu.VMEM((n, HEAD, LANES), BF16),
                pltpu.VMEM((n, tail, LANES), BF16),
                pltpu.VMEM((n * slots, LANES), F32),
                pltpu.VMEM((groups + 1, 2 * GROUP * HEAD, NPAD), BF16),
                pltpu.VMEM((fields, 2 * GROUP * HEAD), BF16),
                pltpu.VMEM((fields, NPAD), F32),
                pltpu.SemaphoreType.DMA((4, 3)),
                pltpu.SemaphoreType.DMA((2,)),
                pltpu.SemaphoreType.DMA((groups,)),
                pltpu.SemaphoreType.DMA,
            ],
            compiler_params=pltpu.CompilerParams(
                collective_id=0, has_side_effects=True, vmem_limit_bytes=60 * 1024 * 1024
            ),
            name="synthesis",
        )(vort, div, leg, wave, points, cosq)

    both = P(("member", "wave"), None, None)
    return jax.shard_map(
        body,
        mesh=mesh,
        in_specs=(both, both, P("wave", None, None), P(None), P("wave"), P("wave")),
        out_specs=both,
        check_vma=False,
    )
```

time: 568 us -> 76.1 us (0.13)
  other arithmetic: 395 us -> 0 us
  waiting for transfers between devices: 73.6 us -> 0 us
  Pallas kernels: 0 us -> 72.4 us
  local copies, waits for them, and re-layouts: 30.9 us -> 2.23 us
  matrix products: 28 us -> 0 us
  blocking collectives: 24.3 us -> 0 us
  starting transfers between devices: 13.4 us -> 0 us
    another operation x6 -> x0, other arithmetic: 371 us -> none
    all_to_all x1 -> x0, waiting for transfers between devices: 73.6 us -> none  [moved_by_axis(): filled = lax.all_to_all(filled, axes[k], k, k, tiled=True)]
    pallas_call x0 -> x1, Pallas kernels: none -> 72.4 us  [body(): pl.pallas_call(functools.partial(kernel, n=n, nwave=nwave), out_shape=jax...]
    dot_general x5 -> x0, matrix products: 28 us -> none  [the longest x4 25.7 us: add_segment(): jnp.einsum('sfrl,rsp->flp', segment, basis, preferred_element_type=jnp.fl...]
    all_to_all x1 -> x0, blocking collectives: 24.3 us -> none  [moved_by_axis(): filled = lax.all_to_all(filled, axes[k], k, k, tiled=True)]
    all_to_all x1 -> x0, starting transfers between devices: 13.4 us -> none  [moved_by_axis(): filled = lax.all_to_all(filled, axes[k], k, k, tiled=True)]
    mul x3 -> x0, other arithmetic: 12.4 us -> none  [the longest x1 6 us: meridional(): return (upper_coef * shifted_up - lower_coef * shifted_down) * live_mask]
    slice x2 -> x0, local copies, waits for them, and re-layouts: 11.5 us -> none  [the longest x1 11.4 us: meridional(): values[..., 1:]]
  transfers between devices with their start and end apart: 1 -> 0, of which waited for: 1 -> 0; matrix products, arithmetic and copies ran while one was open for 0% -> 0% of each run, Pallas kernels for 0% -> 0%
where the time goes in v1:
time: 76.1 us; the launch traced here: 75.9 us
  Pallas kernels  72.4 us (95%)
  local copies, waits for them, and re-layouts  2.23 us (3%)
  between operations  1.3 us (2%)
    pallas_call x1, Pallas kernels, body(): pl.pallas_call(functools.partial(kernel, n=n, nwave=nwave), out_shape=jax...  72.4 us
    unnamed x1, local copies, waits for them, and re-layouts  2.23 us

profile of v1, /device:TPU:37, one launch (start us, length us, event | category | flops | bytes accessed | tf_op | source)
XLA Modules:
  0.0 75.9 jit_solution(14952380303585312029)
XLA Ops:
  1.3 72.4 %synthesis.1 = bf16[1,96,5136]{2,1,0:T(8,128)(2,1)} custom-call(bf16[20,32,1280]{2,1,0:T(8,128)(2,1)} %vort.1, bf16[20,32,1280]{2,1,0:T(8,128)(2,1)} %div.1, bf16[20,64,1280]{2,1,0:T(8,128)(2,1)} %leg.1, s32[1280]{0:T(1024)} %wave.1, s32[1]{0:T(128)S(6)} %copy.8.points, f32[1]{0:T(128)S(6)} %copy.9.cosq), custom_call_target="tpu_custom_call" | custom-call | tf_op jit(solution)/shard_map/synthesis/pallas_call | solution.py:264
  73.7 2.2 %copy.10 = bf16[1,96,5136]{2,1,0:T(8,128)(2,1)} copy(bf16[1,96,5136]{2,1,0:T(8,128)(2,1)} %synthesis.1) | data formatting | bytes 1972224

commit v2 on v1

--- a/solution.py
+++ b/solution.py
@@ -19,19 +19,16 @@
 NT = (((1,), (1,)), ((), ()))
 
 
-def partner(r, z, c, chips, sign):
-    q = r // 2
-    x = r % 2
-    d = jnp.where(q % 2 == 1, (q + 1) // 2, chips - q // 2)
-    chip = (z + 2 * chips + sign * d) % chips
-    return chip * 2 + (c + x) % 2
+def wrapped(chip, chips):
+    chip = jnp.where(chip >= chips, chip - chips, chip)
+    return jnp.where(chip < 0, chip + chips, chip)
 
 
 def kernel(
     vort, div, leg, wave, points, cosq, out,
     spec, legv, mown, coef_a, coef_b, coef_c, res,
-    send_a, send_b, recv_a, recv_b, mb, basis, fields, acc,
-    in_sem, ssem, rsem_a, rsem_b,
+    send_a, send_b, recv_a, recv_b, mb, basis, qrow, fields, acc,
+    in_sem, ssem, rsem_a, rsem_b, far,
     *, n, nwave,
 ):
     w = lax.axis_index("wave")
@@ -56,19 +53,25 @@
             pltpu.make_async_copy(leg.at[at], legv.at[at], in_sem.at[g, 2]),
         )
 
-    for g in range(steps):
+    for g in (steps - 1, *range(steps - 1)):
         for copy in loads(g):
             copy.start()
 
     barrier = pltpu.get_barrier_semaphore()
-
-    def greet(r, carry):
-        pl.semaphore_signal(
-            barrier, inc=1, device_id={"wave": partner(r, z, c, chips, -1)}, device_id_type=MESH
-        )
+    near = chips // 4
+
+    def hello(dev):
+        pl.semaphore_signal(barrier, inc=1, device_id={"wave": dev}, device_id_type=MESH)
+
+    hello(2 * z + 1 - c)
+
+    def greet(k, carry):
+        for chip in (wrapped(z - k, chips), wrapped(z + k, chips)):
+            hello(2 * chip)
+            hello(2 * chip + 1)
         return carry
 
-    lax.fori_loop(1, n, greet, 0)
+    lax.fori_loop(1, near + 1, greet, 0)
 
     mown[...] = jnp.zeros_like(mown)
     for s in range(slots):
@@ -90,8 +93,9 @@
         coef_c[:, cols] = jnp.where(live & (deg >= 2.0), coupled(safe), 0.0)
 
     lane16 = lax.broadcasted_iota(jnp.int32, (16, nwave), 1)
-
-    def one_slot(s, carry):
+    pitch = n + 8
+
+    def one_slot(s):
         m = wave[w * slots + s]
         a = coef_a[pl.ds(s, 1), :]
         b = coef_b[pl.ds(s, 1), :]
@@ -110,58 +114,76 @@
         mask = jnp.where(lane16 < nwave - m, 1.0, 0.0).astype(BF16)
         values = legv[s]
         masked = jnp.concatenate([values[16 * i : 16 * i + 16] * mask for i in range(n // 16)], axis=0)
-        res[pl.ds(pl.multiple_of(s * n, n), n), :] = lax.dot_general(
+        res[pl.ds(pl.multiple_of(s * pitch, 8), n), :] = lax.dot_general(
             masked, spec[s], NT, preferred_element_type=F32
         )
-        return carry
-
-    for g in range(steps):
+
+    def quad(g, carry):
         for copy in loads(g):
             copy.wait()
-        lax.fori_loop(g * per, (g + 1) * per, one_slot, 0)
-
-    def pack(r, carry):
-        dst = partner(r, z, c, chips, -1)
-        send_a[r] = res[pl.ds(dst, HEAD, stride=n), :].astype(BF16)
-        send_b[r] = res[pl.ds(HEAD * n + dst, tail, stride=n), :].astype(BF16)
+        for u in range(per):
+            one_slot(g * per + u)
         return carry
 
-    lax.fori_loop(0, n, pack, 0)
-    recv_a[0] = send_a[0]
-    recv_b[0] = send_b[0]
-
-    pl.semaphore_wait(barrier, n - 1)
-
-    def post_b(j, carry):
-        r = n - 1 - j
+    def post(src, dst, rsem, ssem, r, dev):
         pltpu.make_async_remote_copy(
-            src_ref=send_b.at[r], dst_ref=recv_b.at[r], send_sem=ssem.at[1], recv_sem=rsem_b,
-            device_id={"wave": partner(r, z, c, chips, -1)}, device_id_type=MESH,
+            src_ref=src.at[dev], dst_ref=dst.at[r], send_sem=ssem, recv_sem=rsem,
+            device_id={"wave": dev}, device_id_type=MESH,
         ).start()
-        return carry
-
-    def post_a(j, carry):
-        r = n - 1 - j
-        pltpu.make_async_remote_copy(
-            src_ref=send_a.at[r], dst_ref=recv_a.at[r], send_sem=ssem.at[0], recv_sem=rsem_a.at[r // GROUP],
-            device_id={"wave": partner(r, z, c, chips, -1)}, device_id_type=MESH,
-        ).start()
-        return carry
-
-    lax.fori_loop(0, n - 1, post_b, 0)
-    lax.fori_loop(0, n - 1, post_a, 0)
-
-    def place(r, carry):
-        base = partner(r, z, c, chips, 1) * slots
+
+    def post_b(r, dev):
+        post(send_b, recv_b, rsem_b, ssem.at[1], r, dev)
+
+    def post_a(r, dev):
+        post(send_a, recv_a, rsem_a.at[r // GROUP], ssem.at[0], r, dev)
+
+    def outward(send, high, low):
+        def trip(j, carry):
+            k = high - j
+            for q, chip in ((2 * k - 1, wrapped(z - k, chips)), (2 * k, wrapped(z + k, chips))):
+                send(2 * q, 2 * chip + c)
+                send(2 * q + 1, 2 * chip + 1 - c)
+            return carry
+
+        lax.fori_loop(0, high - low + 1, trip, 0)
+
+    def across(send):
+        chip = wrapped(z + chips // 2, chips)
+        send(2 * (chips - 1), 2 * chip + c)
+        send(2 * (chips - 1) + 1, 2 * chip + 1 - c)
+
+    quad(steps - 1, 0)
+    for dev in range(n):
+        send_b[dev] = res[pl.ds(HEAD * pitch + dev, tail, stride=pitch), :].astype(BF16)
+    recv_b[0] = send_b[w]
+    lax.fori_loop(0, steps - 1, quad, 0)
+    for dev in range(n):
+        send_a[dev] = res[pl.ds(dev, HEAD, stride=pitch), :].astype(BF16)
+    recv_a[0] = send_a[w]
+
+    pl.semaphore_wait(barrier, 2 * (2 * near + 1) - 1)
+    for chip in (wrapped(z - near, chips), wrapped(z + near, chips)):
+        pl.semaphore_signal(far, inc=1, device_id={"wave": 2 * chip + c}, device_id_type=MESH)
+    outward(post_b, near, 1)
+    outward(post_a, near, near - 1)
+
+    def rows_of(r, dev):
+        base = dev * slots
         for s in range(HEAD):
             mb[pl.ds(r * HEAD + s, 1), :] = jnp.full((1, LANES), wave[base + s].astype(F32), F32)
         for s in range(tail):
             mb[pl.ds(n * HEAD + r * tail + s, 1), :] = jnp.full(
                 (1, LANES), wave[base + HEAD + s].astype(F32), F32
             )
+
+    def place(q, carry):
+        d = jnp.where(q % 2 == 1, (q + 1) // 2, -(q // 2))
+        chip = wrapped(z + d, chips)
+        rows_of(2 * q, 2 * chip + c)
+        rows_of(2 * q + 1, 2 * chip + 1 - c)
         return carry
 
-    lax.fori_loop(0, n, place, 0)
+    lax.fori_loop(0, chips, place, 0)
 
     count = points[0].astype(F32)
     pv = jnp.full((1, LANES), count, F32)
@@ -197,7 +219,19 @@
             cv, sv = cv * cr + sv * sr, sv * cr - cv * sr
         return carry
 
-    lax.fori_loop(0, mb.shape[0] // span, make_basis, 0)
+    trips = mb.shape[0] // span
+    lax.fori_loop(groups * (ka // span), trips, make_basis, 0)
+
+    pl.semaphore_wait(far, 2)
+    across(post_b)
+    outward(post_b, chips // 2 - 1, near + 1)
+    across(post_a)
+    outward(post_a, chips // 2 - 1, near + 1)
+    outward(post_a, near - 2, 1)
+    post_b(1, 2 * z + 1 - c)
+    post_a(1, 2 * z + 1 - c)
+
+    lax.fori_loop(0, groups * (ka // span), make_basis, 0)
 
     eye = (
         lax.broadcasted_iota(jnp.int32, (LANES, LANES), 0) == lax.broadcasted_iota(jnp.int32, (LANES, LANES), 1)
@@ -205,11 +239,13 @@
     first = (lax.broadcasted_iota(jnp.int32, (8, LANES), 1) == 0).astype(F32)
     inv_c = 1.0 / jnp.full((1, ka), cosq[0], F32)
 
+    for g in range(groups + 1):
+        qrow[g] = lax.dot_general(
+            first, mb[pl.ds(g * ka, ka), :], NT, precision=lax.Precision.HIGHEST, preferred_element_type=F32
+        ) / radius
+
     def derive(g, arrived):
-        mrow = lax.dot_general(
-            first, mb[pl.ds(g * ka, ka), :], NT, precision=lax.Precision.HIGHEST, preferred_element_type=F32
-        )
-        q = mrow[0:1] / radius
+        q = qrow[g, 0:1, :]
         x = lax.dot_general(eye, arrived, NT, preferred_element_type=F32)
         ur, ui, vr, vi, zr, zi, dr, di = (x[half * i : half * (i + 1)] for i in range(8))
         for side, (u, v, ul, vl, zt, dl) in enumerate(
@@ -257,7 +293,7 @@
         slots, rows, nwave = vort.shape
         tail = slots - HEAD
         fields = 12 * rows // 4
-        hbm = pl.BlockSpec(memory_space=pl.ANY)
+        hbm = pl.BlockSpec(memory_space=pltpu.MemorySpace.HBM)
         smem = pl.BlockSpec(memory_space=pltpu.SMEM)
         groups = n // GROUP
         own = -(-slots // 8) * 8
@@ -273,25 +309,27 @@
                 pltpu.VMEM((own, nwave), F32),
                 pltpu.VMEM((own, nwave), F32),
                 pltpu.VMEM((own, nwave), F32),
-                pltpu.VMEM((slots * n, LANES), F32),
+                pltpu.VMEM((slots * (n + 8), LANES), F32),
                 pltpu.VMEM((n, HEAD, LANES), BF16),
                 pltpu.VMEM((n, tail, LANES), BF16),
                 pltpu.VMEM((n, HEAD, LANES), BF16),
                 pltpu.VMEM((n, tail, LANES), BF16),
                 pltpu.VMEM((n * slots, LANES), F32),
                 pltpu.VMEM((groups + 1, 2 * GROUP * HEAD, NPAD), BF16),
+                pltpu.VMEM((groups + 1, 8, GROUP * HEAD), F32),
                 pltpu.VMEM((fields, 2 * GROUP * HEAD), BF16),
                 pltpu.VMEM((fields, NPAD), F32),
-                pltpu.SemaphoreType.DMA((4, 3)),
+                pltpu.SemaphoreType.DMA((slots // tail, 3)),
                 pltpu.SemaphoreType.DMA((2,)),
                 pltpu.SemaphoreType.DMA((groups,)),
                 pltpu.SemaphoreType.DMA,
+                pltpu.SemaphoreType.REGULAR,
             ],
             compiler_params=pltpu.CompilerParams(
-                collective_id=0, has_side_effects=True, vmem_limit_bytes=60 * 1024 * 1024
+                collective_id=0, has_side_effects=True, vmem_limit_bytes=46 * 1024 * 1024
             ),
             name="synthesis",
-        )(vort, div, leg, wave, points, cosq)
+        )(*(pltpu.with_memory_space_constraint(v, pltpu.MemorySpace.HBM) for v in (vort, div, leg, wave)), points, cosq)
 
     both = P(("member", "wave"), None, None)
     return jax.shard_map(

time: 76.1 us -> 69 us (0.907)
  Pallas kernels: 72.4 us -> 66.6 us
  local copies, waits for them, and re-layouts: 2.23 us -> 0.95 us
    pallas_call x1, Pallas kernels: 72.4 us -> 66.6 us  [body(): pl.pallas_call(functools.partial(kernel, n=n, nwave=nwave), out_shape=jax...]
    unnamed x1, local copies, waits for them, and re-layouts: 2.23 us -> 0.95 us
where the time goes in v2:
time: 69 us; the launch traced here: 68.8 us
  Pallas kernels  66.6 us (97%)
  between operations  1.3 us (2%)
  local copies, waits for them, and re-layouts  0.95 us (1%)
    pallas_call x1, Pallas kernels, body(): pl.pallas_call(functools.partial(kernel, n=n, nwave=nwave), out_shape=jax...  66.6 us

profile of v2, /device:TPU:37, one launch (start us, length us, event | category | flops | bytes accessed | tf_op | source)
XLA Modules:
  0.0 68.8 jit_solution(14792606559291856637)
XLA Ops:
  1.3 66.6 %synthesis.1 = bf16[1,96,5136]{2,1,0:T(8,128)(2,1)S(1)} custom-call(bf16[20,32,1280]{2,1,0:T(8,128)(2,1)} %vort.1, bf16[20,32,1280]{2,1,0:T(8,128)(2,1)} %div.1, bf16[20,64,1280]{2,1,0:T(8,128)(2,1)} %leg.1, s32[1280]{0:T(1024)} %wave.1, s32[1]{0:T(128)S(6)} %copy.8.points, f32[1]{0:T(128)S(6)} %copy.9.cosq), custom_call_target="tpu_custom_call" | custom-call | tf_op jit(solution)/shard_map/synthesis/pallas_call | solution.py:300
  67.9 1.0 %copy.10 = bf16[1,96,5136]{2,1,0:T(8,128)(2,1)} copy(bf16[1,96,5136]{2,1,0:T(8,128)(2,1)S(1)} %synthesis.1) | data formatting | bytes 1972224

commit v3 on v2

--- a/solution.py
+++ b/solution.py
@@ -164,8 +164,10 @@
     pl.semaphore_wait(barrier, 2 * (2 * near + 1) - 1)
     for chip in (wrapped(z - near, chips), wrapped(z + near, chips)):
         pl.semaphore_signal(far, inc=1, device_id={"wave": 2 * chip + c}, device_id_type=MESH)
+    outward(post_a, near, 1)
     outward(post_b, near, 1)
-    outward(post_a, near, near - 1)
+    post_a(1, 2 * z + 1 - c)
+    post_b(1, 2 * z + 1 - c)
 
     def rows_of(r, dev):
         base = dev * slots
@@ -223,13 +225,10 @@
     lax.fori_loop(groups * (ka // span), trips, make_basis, 0)
 
     pl.semaphore_wait(far, 2)
+    across(post_a)
     across(post_b)
     outward(post_b, chips // 2 - 1, near + 1)
-    across(post_a)
     outward(post_a, chips // 2 - 1, near + 1)
-    outward(post_a, near - 2, 1)
-    post_b(1, 2 * z + 1 - c)
-    post_a(1, 2 * z + 1 - c)
 
     lax.fori_loop(0, groups * (ka // span), make_basis, 0)
 
@@ -264,20 +263,27 @@
 
         lax.fori_loop(0, NPAD // NBLOCK, column, 0)
 
-    pltpu.make_async_copy(recv_b.at[pl.ds(1, n - 1)], recv_b.at[pl.ds(1, n - 1)], rsem_b).wait()
-    derive(groups, recv_b[...].reshape(n * tail, LANES))
-    accumulate(groups, True)
-    for g in range(groups - 1, -1, -1):
+    def quarter(g):
         at = pl.ds(1, GROUP - 1) if g == 0 else pl.ds(g * GROUP, GROUP)
         pltpu.make_async_copy(recv_a.at[at], recv_a.at[at], rsem_a.at[g]).wait()
         derive(g, recv_a[pl.ds(g * GROUP, GROUP)].reshape(ka, LANES))
-        if g > 0:
-            accumulate(g, False)
+
+    last = groups // 2
+    for g in range(last):
+        quarter(g)
+        accumulate(g, g == 0)
+    pltpu.make_async_copy(recv_b.at[pl.ds(1, n - 1)], recv_b.at[pl.ds(1, n - 1)], rsem_b).wait()
+    derive(groups, recv_b[...].reshape(n * tail, LANES))
+    accumulate(groups, False)
+    for g in range(groups - 1, last, -1):
+        quarter(g)
+        accumulate(g, False)
+    quarter(last)
 
     for j in range(NPAD // NBLOCK):
         lo = j * NBLOCK
         hi = min(lo + NBLOCK, NLON)
-        new = jnp.dot(fields[...], basis[0, :, lo : lo + NBLOCK], preferred_element_type=F32)
+        new = jnp.dot(fields[...], basis[last, :, lo : lo + NBLOCK], preferred_element_type=F32)
         total = acc[:, lo : lo + NBLOCK] + new
         pos = lax.broadcasted_iota(jnp.int32, total.shape, 1) + lo
         out[0, :, lo:hi] = jnp.where(pos < points[0], total, 0.0).astype(BF16)[:, : hi - lo]

time: 69 us -> 67.1 us (0.972)
  Pallas kernels: 66.6 us -> 64.7 us
    pallas_call x1, Pallas kernels: 66.6 us -> 64.7 us  [body(): pl.pallas_call(functools.partial(kernel, n=n, nwave=nwave), out_shape=jax...]
where the time goes in v3:
time: 67.1 us; the launch traced here: 67 us
  Pallas kernels  64.7 us (96%)
  between operations  1.3 us (2%)
  local copies, waits for them, and re-layouts  0.95 us (1%)
    pallas_call x1, Pallas kernels, body(): pl.pallas_call(functools.partial(kernel, n=n, nwave=nwave), out_shape=jax...  64.7 us

profile of v3, /device:TPU:37, one launch (start us, length us, event | category | flops | bytes accessed | tf_op | source)
XLA Modules:
  0.0 67.0 jit_solution(2595519532165506804)
XLA Ops:
  1.3 64.7 %synthesis.1 = bf16[1,96,5136]{2,1,0:T(8,128)(2,1)S(1)} custom-call(bf16[20,32,1280]{2,1,0:T(8,128)(2,1)} %vort.1, bf16[20,32,1280]{2,1,0:T(8,128)(2,1)} %div.1, bf16[20,64,1280]{2,1,0:T(8,128)(2,1)} %leg.1, s32[1280]{0:T(1024)} %wave.1, s32[1]{0:T(128)S(6)} %copy.8.points, f32[1]{0:T(128)S(6)} %copy.9.cosq), custom_call_target="tpu_custom_call" | custom-call | tf_op jit(solution)/shard_map/synthesis/pallas_call | solution.py:306
  66.0 1.0 %copy.10 = bf16[1,96,5136]{2,1,0:T(8,128)(2,1)} copy(bf16[1,96,5136]{2,1,0:T(8,128)(2,1)S(1)} %synthesis.1) | data formatting | bytes 1972224

commit v4 on v3

--- a/solution.py
+++ b/solution.py
@@ -25,10 +25,11 @@
 
 
 def kernel(
-    vort, div, leg, wave, points, cosq, out,
+    vort, div, leg, wave_in, points, cosq, out,
+    wave,
     spec, legv, mown, coef_a, coef_b, coef_c, res,
     send_a, send_b, recv_a, recv_b, mb, basis, qrow, fields, acc,
-    in_sem, ssem, rsem_a, rsem_b, far,
+    in_sem, small_sem, ssem, rsem_a, rsem_b, far,
     *, n, nwave,
 ):
     w = lax.axis_index("wave")
@@ -53,6 +54,8 @@
             pltpu.make_async_copy(leg.at[at], legv.at[at], in_sem.at[g, 2]),
         )
 
+    waves = pltpu.make_async_copy(wave_in, wave, small_sem)
+    waves.start()
     for g in (steps - 1, *range(steps - 1)):
         for copy in loads(g):
             copy.start()
@@ -63,15 +66,16 @@
     def hello(dev):
         pl.semaphore_signal(barrier, inc=1, device_id={"wave": dev}, device_id_type=MESH)
 
-    hello(2 * z + 1 - c)
-
-    def greet(k, carry):
+    def greet(j, carry):
+        k = near - j
         for chip in (wrapped(z - k, chips), wrapped(z + k, chips)):
             hello(2 * chip)
             hello(2 * chip + 1)
         return carry
 
-    lax.fori_loop(1, near + 1, greet, 0)
+    lax.fori_loop(0, near, greet, 0)
+    hello(2 * z + 1 - c)
+    waves.wait()
 
     mown[...] = jnp.zeros_like(mown)
     for s in range(slots):
@@ -306,9 +310,10 @@
         return pl.pallas_call(
             functools.partial(kernel, n=n, nwave=nwave),
             out_shape=jax.ShapeDtypeStruct((1, fields, NLON), BF16),
-            in_specs=[hbm, hbm, hbm, smem, smem, smem],
+            in_specs=[hbm, hbm, hbm, hbm, smem, smem],
             out_specs=pl.BlockSpec(memory_space=pltpu.VMEM),
             scratch_shapes=[
+                pltpu.SMEM(wave.shape, wave.dtype),
                 pltpu.VMEM((slots, 4 * rows, nwave), BF16),
                 pltpu.VMEM((slots, n, nwave), BF16),
                 pltpu.VMEM((own, LANES), F32),
@@ -326,6 +331,7 @@
                 pltpu.VMEM((fields, 2 * GROUP * HEAD), BF16),
                 pltpu.VMEM((fields, NPAD), F32),
                 pltpu.SemaphoreType.DMA((slots // tail, 3)),
+                pltpu.SemaphoreType.DMA,
                 pltpu.SemaphoreType.DMA((2,)),
                 pltpu.SemaphoreType.DMA((groups,)),
                 pltpu.SemaphoreType.DMA,

time: 67.1 us -> 66.4 us (0.990)
  Pallas kernels: 64.7 us -> 64 us
    pallas_call x1, Pallas kernels: 64.7 us -> 64 us  [body(): pl.pallas_call(functools.partial(kernel, n=n, nwave=nwave), out_shape=jax...]
where the time goes in v4:
time: 66.4 us; the launch traced here: 66.3 us
  Pallas kernels  64 us (96%)
  between operations  1.3 us (2%)
  local copies, waits for them, and re-layouts  0.95 us (1%)
    pallas_call x1, Pallas kernels, body(): pl.pallas_call(functools.partial(kernel, n=n, nwave=nwave), out_shape=jax...  64 us

profile of v4, /device:TPU:37, one launch (start us, length us, event | category | flops | bytes accessed | tf_op | source)
XLA Modules:
  0.0 66.3 jit_solution(4350671225798565014)
XLA Ops:
  1.3 64.0 %synthesis.1 = bf16[1,96,5136]{2,1,0:T(8,128)(2,1)S(1)} custom-call(bf16[20,32,1280]{2,1,0:T(8,128)(2,1)} %vort.1, bf16[20,32,1280]{2,1,0:T(8,128)(2,1)} %div.1, bf16[20,64,1280]{2,1,0:T(8,128)(2,1)} %leg.1, s32[1280]{0:T(1024)} %wave_in.1, s32[1]{0:T(128)S(6)} %copy.8.points, f32[1]{0:T(128)S(6)} %copy.9.cosq), custom_call_target="tpu_custom_call" | custom-call | tf_op jit(solution)/shard_map/synthesis/pallas_call | solution.py:310
  65.3 1.0 %copy.10 = bf16[1,96,5136]{2,1,0:T(8,128)(2,1)} copy(bf16[1,96,5136]{2,1,0:T(8,128)(2,1)S(1)} %synthesis.1) | data formatting | bytes 1972224

commit v5 on v4

--- a/solution.py
+++ b/solution.py
@@ -109,11 +109,11 @@
             x = spec[s, pl.ds(2 * rows + half * i, half), :].astype(F32)
             up = pltpu.roll(x, nwave - 1, 1)
             down = pltpu.roll(x, 1, 1)
-            parts.append((x * a, up * b - down * cc))
+            parts.append((x * a, down * cc - up * b if i < 2 else up * b - down * cc))
         (zr, hzr), (zi, hzi), (dr, hdr), (di, hdi) = parts
-        spec[s, pl.ds(0, half), :] = (-di - hzr).astype(BF16)
-        spec[s, pl.ds(half, half), :] = (dr - hzi).astype(BF16)
-        spec[s, pl.ds(2 * half, half), :] = (-zi + hdr).astype(BF16)
+        spec[s, pl.ds(0, half), :] = (hzr - di).astype(BF16)
+        spec[s, pl.ds(half, half), :] = (dr + hzi).astype(BF16)
+        spec[s, pl.ds(2 * half, half), :] = (hdr - zi).astype(BF16)
         spec[s, pl.ds(3 * half, half), :] = (zr + hdi).astype(BF16)
         mask = jnp.where(lane16 < nwave - m, 1.0, 0.0).astype(BF16)
         values = legv[s]
@@ -168,7 +168,8 @@
     pl.semaphore_wait(barrier, 2 * (2 * near + 1) - 1)
     for chip in (wrapped(z - near, chips), wrapped(z + near, chips)):
         pl.semaphore_signal(far, inc=1, device_id={"wave": 2 * chip + c}, device_id_type=MESH)
-    outward(post_a, near, 1)
+    held = near // 2
+    outward(post_a, near, held + 1)
     outward(post_b, near, 1)
     post_a(1, 2 * z + 1 - c)
     post_b(1, 2 * z + 1 - c)
@@ -273,13 +274,11 @@
         derive(g, recv_a[pl.ds(g * GROUP, GROUP)].reshape(ka, LANES))
 
     last = groups // 2
-    for g in range(last):
-        quarter(g)
-        accumulate(g, g == 0)
     pltpu.make_async_copy(recv_b.at[pl.ds(1, n - 1)], recv_b.at[pl.ds(1, n - 1)], rsem_b).wait()
+    outward(post_a, held, 1)
     derive(groups, recv_b[...].reshape(n * tail, LANES))
-    accumulate(groups, False)
-    for g in range(groups - 1, last, -1):
+    accumulate(groups, True)
+    for g in (*range(last - 1, -1, -1), *range(groups - 1, last, -1)):
         quarter(g)
         accumulate(g, False)
     quarter(last)

time: 66.4 us -> 67.1 us (1.011)
  Pallas kernels: 64 us -> 64.8 us
    pallas_call x1, Pallas kernels: 64 us -> 64.8 us  [body(): pl.pallas_call(functools.partial(kernel, n=n, nwave=nwave), out_shape=jax...]
where the time goes in v5:
time: 67.1 us; the launch traced here: 67 us
  Pallas kernels  64.8 us (97%)
  between operations  1.3 us (2%)
  local copies, waits for them, and re-layouts  0.95 us (1%)
    pallas_call x1, Pallas kernels, body(): pl.pallas_call(functools.partial(kernel, n=n, nwave=nwave), out_shape=jax...  64.8 us

profile of v5, /device:TPU:37, one launch (start us, length us, event | category | flops | bytes accessed | tf_op | source)
XLA Modules:
  0.0 67.0 jit_solution(15234396418570951054)
XLA Ops:
  1.3 64.8 %synthesis.1 = bf16[1,96,5136]{2,1,0:T(8,128)(2,1)S(1)} custom-call(bf16[20,32,1280]{2,1,0:T(8,128)(2,1)} %vort.1, bf16[20,32,1280]{2,1,0:T(8,128)(2,1)} %div.1, bf16[20,64,1280]{2,1,0:T(8,128)(2,1)} %leg.1, s32[1280]{0:T(1024)} %wave_in.1, s32[1]{0:T(128)S(6)} %copy.8.points, f32[1]{0:T(128)S(6)} %copy.9.cosq), custom_call_target="tpu_custom_call" | custom-call | tf_op jit(solution)/shard_map/synthesis/pallas_call | solution.py:309
  66.1 1.0 %copy.10 = bf16[1,96,5136]{2,1,0:T(8,128)(2,1)} copy(bf16[1,96,5136]{2,1,0:T(8,128)(2,1)S(1)} %synthesis.1) | data formatting | bytes 1972224

commit v6 on v5

--- a/solution.py
+++ b/solution.py
@@ -168,7 +168,7 @@
     pl.semaphore_wait(barrier, 2 * (2 * near + 1) - 1)
     for chip in (wrapped(z - near, chips), wrapped(z + near, chips)):
         pl.semaphore_signal(far, inc=1, device_id={"wave": 2 * chip + c}, device_id_type=MESH)
-    held = near // 2
+    held = near // 2 - 1
     outward(post_a, near, held + 1)
     outward(post_b, near, 1)
     post_a(1, 2 * z + 1 - c)
@@ -234,6 +234,7 @@
     across(post_b)
     outward(post_b, chips // 2 - 1, near + 1)
     outward(post_a, chips // 2 - 1, near + 1)
+    outward(post_a, held, 1)
 
     lax.fori_loop(0, groups * (ka // span), make_basis, 0)
 
@@ -273,12 +274,13 @@
         pltpu.make_async_copy(recv_a.at[at], recv_a.at[at], rsem_a.at[g]).wait()
         derive(g, recv_a[pl.ds(g * GROUP, GROUP)].reshape(ka, LANES))
 
-    last = groups // 2
+    last = 0
+    quarter(1)
+    accumulate(1, True)
     pltpu.make_async_copy(recv_b.at[pl.ds(1, n - 1)], recv_b.at[pl.ds(1, n - 1)], rsem_b).wait()
-    outward(post_a, held, 1)
     derive(groups, recv_b[...].reshape(n * tail, LANES))
-    accumulate(groups, True)
-    for g in (*range(last - 1, -1, -1), *range(groups - 1, last, -1)):
+    accumulate(groups, False)
+    for g in range(groups - 1, 1, -1):
         quarter(g)
         accumulate(g, False)
     quarter(last)

time: 67.1 us -> 68 us (1.013)
  Pallas kernels: 64.8 us -> 65.6 us
    pallas_call x1, Pallas kernels: 64.8 us -> 65.6 us  [body(): pl.pallas_call(functools.partial(kernel, n=n, nwave=nwave), out_shape=jax...]
where the time goes in v6:
time: 68 us; the launch traced here: 67.9 us
  Pallas kernels  65.6 us (96%)
  between operations  1.3 us (2%)
  local copies, waits for them, and re-layouts  0.95 us (1%)
    pallas_call x1, Pallas kernels, body(): pl.pallas_call(functools.partial(kernel, n=n, nwave=nwave), out_shape=jax...  65.6 us

profile of v6, /device:TPU:37, one launch (start us, length us, event | category | flops | bytes accessed | tf_op | source)
XLA Modules:
  0.0 67.9 jit_solution(2789867427567717598)
XLA Ops:
  1.3 65.6 %synthesis.1 = bf16[1,96,5136]{2,1,0:T(8,128)(2,1)S(1)} custom-call(bf16[20,32,1280]{2,1,0:T(8,128)(2,1)} %vort.1, bf16[20,32,1280]{2,1,0:T(8,128)(2,1)} %div.1, bf16[20,64,1280]{2,1,0:T(8,128)(2,1)} %leg.1, s32[1280]{0:T(1024)} %wave_in.1, s32[1]{0:T(128)S(6)} %copy.8.points, f32[1]{0:T(128)S(6)} %copy.9.cosq), custom_call_target="tpu_custom_call" | custom-call | tf_op jit(solution)/shard_map/synthesis/pallas_call | solution.py:311
  66.9 1.0 %copy.10 = bf16[1,96,5136]{2,1,0:T(8,128)(2,1)} copy(bf16[1,96,5136]{2,1,0:T(8,128)(2,1)S(1)} %synthesis.1) | data formatting | bytes 1972224

commit v7 on v4

--- a/solution.py
+++ b/solution.py
@@ -56,9 +56,8 @@
 
     waves = pltpu.make_async_copy(wave_in, wave, small_sem)
     waves.start()
-    for g in (steps - 1, *range(steps - 1)):
-        for copy in loads(g):
-            copy.start()
+    for copy in loads(steps - 1):
+        copy.start()
 
     barrier = pltpu.get_barrier_semaphore()
     near = chips // 4
@@ -73,7 +72,11 @@
             hello(2 * chip + 1)
         return carry
 
-    lax.fori_loop(0, near, greet, 0)
+    greet(0, 0)
+    for g in range(steps - 1):
+        for copy in loads(g):
+            copy.start()
+    lax.fori_loop(1, near, greet, 0)
     hello(2 * z + 1 - c)
     waves.wait()
 
@@ -109,11 +112,11 @@
             x = spec[s, pl.ds(2 * rows + half * i, half), :].astype(F32)
             up = pltpu.roll(x, nwave - 1, 1)
             down = pltpu.roll(x, 1, 1)
-            parts.append((x * a, up * b - down * cc))
+            parts.append((x * a, down * cc - up * b if i < 2 else up * b - down * cc))
         (zr, hzr), (zi, hzi), (dr, hdr), (di, hdi) = parts
-        spec[s, pl.ds(0, half), :] = (-di - hzr).astype(BF16)
-        spec[s, pl.ds(half, half), :] = (dr - hzi).astype(BF16)
-        spec[s, pl.ds(2 * half, half), :] = (-zi + hdr).astype(BF16)
+        spec[s, pl.ds(0, half), :] = (hzr - di).astype(BF16)
+        spec[s, pl.ds(half, half), :] = (dr + hzi).astype(BF16)
+        spec[s, pl.ds(2 * half, half), :] = (hdr - zi).astype(BF16)
         spec[s, pl.ds(3 * half, half), :] = (zr + hdi).astype(BF16)
         mask = jnp.where(lane16 < nwave - m, 1.0, 0.0).astype(BF16)
         values = legv[s]

time: 66.4 us -> 66.4 us (level)
  no operation moved by 1% of the time
where the time goes in v7:
time: 66.4 us; the launch traced here: 66.3 us
  Pallas kernels  64 us (96%)
  between operations  1.3 us (2%)
  local copies, waits for them, and re-layouts  0.95 us (1%)
    pallas_call x1, Pallas kernels, body(): pl.pallas_call(functools.partial(kernel, n=n, nwave=nwave), out_shape=jax...  64 us

profile of v7, /device:TPU:37, one launch (start us, length us, event | category | flops | bytes accessed | tf_op | source)
XLA Modules:
  0.0 66.3 jit_solution(14439698230406046109)
XLA Ops:
  1.3 64.0 %synthesis.1 = bf16[1,96,5136]{2,1,0:T(8,128)(2,1)S(1)} custom-call(bf16[20,32,1280]{2,1,0:T(8,128)(2,1)} %vort.1, bf16[20,32,1280]{2,1,0:T(8,128)(2,1)} %div.1, bf16[20,64,1280]{2,1,0:T(8,128)(2,1)} %leg.1, s32[1280]{0:T(1024)} %wave_in.1, s32[1]{0:T(128)S(6)} %copy.8.points, f32[1]{0:T(128)S(6)} %copy.9.cosq), custom_call_target="tpu_custom_call" | custom-call | tf_op jit(solution)/shard_map/synthesis/pallas_call | solution.py:313
  65.3 1.0 %copy.10 = bf16[1,96,5136]{2,1,0:T(8,128)(2,1)} copy(bf16[1,96,5136]{2,1,0:T(8,128)(2,1)S(1)} %synthesis.1) | data formatting | bytes 1972224
